TPU v7x, 32 devices: a whole 2x2x4 slice. The times are simulated.
32 devices in a mesh: dp: 8 (over z, y), mp: 4 (over x, core).
Axes of the slice: x: 2, y: 2, z: 4, core: 2. Of those that a mesh axis runs over, the one named last changes fastest.
Arguments:
- picture_skip_activations: bfloat16 [16384, 1152], P('dp'), as said below
- caption_closing_activations: bfloat16 [64, 1152], P('dp'), as said below
- normaliser_multipliers: float32 [3, 1152], replicated, may hold values from 0.1 to 1.9
- widening_matrix: bfloat16 [1152, 4304], P('dp', 'mp'), may hold values from -0.1875 to 0.1875
- contracting_matrix: bfloat16 [4304, 1152], P('mp', 'dp'), as said below
- caption_mapping_matrix: bfloat16 [1152, 1152], replicated, as said below
- sharpness_factor: float32 [1], replicated, may hold values from 8 to 32
- score_offset_term: float32 [1], replicated, may hold values from -8 to -3
Outputs:
- row_loss: float32 [64], P('dp')
- col_loss: float32 [64], P('dp')
Inputs may be any that keep to these rules, and one draw needn't show every extreme that they name: `picture_skip_activations`: entries lie within -8 and 8. `caption_closing_activations`: entries lie within -8 and 8. `contracting_matrix`: entries are at most 4.4 / sqrt(4304) in magnitude. `caption_mapping_matrix`: diagonal entries lie within 1 - 2.1 / sqrt(1152) and 1 + 2.1 / sqrt(1152), the others within -2.1 / sqrt(1152) and 2.1 / sqrt(1152).
All inputs are finite; a program needn't handle non-finite values.
Results may differ from a plain program's by a relative error of at most 0.01.
Values may be sent and summed in bfloat16 or wider, within the bound.
A program may use at most 128 MiB of HBM per device.

v0:
```python
import jax
import jax.numpy as jnp
from jax import lax
from jax.sharding import PartitionSpec as P

PATCHES = 256


def layer_norm(values, norm_gain):
    average = jnp.mean(values, axis=-1, keepdims=True)
    centred = values - average
    spread = jnp.mean(centred * centred, axis=-1, keepdims=True)
    return centred * lax.rsqrt(spread + 1e-06) * norm_gain


def unit_vector(vector):
    length = jnp.sqrt(jnp.sum(vector * vector, axis=-1, keepdims=True))
    return (vector / jnp.maximum(length, 1.0)).astype(jnp.bfloat16)


def pool_images(image_final):
    return jnp.mean(image_final.reshape(-1, PATCHES, image_final.shape[1]), axis=1)


def on_device(
    picture_skip_activations,
    caption_closing_activations,
    normaliser_multipliers,
    widening_matrix,
    contracting_matrix,
    caption_mapping_matrix,
    sharpness_factor,
    score_offset_term,
):
    image_rows = picture_skip_activations.astype(jnp.float32)
    image_normed = layer_norm(image_rows, normaliser_multipliers[0]).astype(jnp.bfloat16)
    inner_weight = lax.all_gather(widening_matrix, "dp", axis=0, tiled=True)
    image_units = jax.nn.gelu(
        jnp.dot(image_normed, inner_weight, preferred_element_type=jnp.float32), approximate=True
    ).astype(jnp.bfloat16)
    partial_out = jnp.dot(
        image_units,
        lax.all_gather(contracting_matrix, "dp", axis=1, tiled=True),
        preferred_element_type=jnp.float32,
    )
    unit_share = lax.psum_scatter(
        partial_out.astype(jnp.bfloat16), "mp", scatter_dimension=0, tiled=True
    ).astype(jnp.float32)
    own_count = unit_share.shape[0]
    own_first = lax.axis_index("mp") * own_count
    own_rows = lax.dynamic_slice_in_dim(image_rows, own_first, own_count, 0)
    image_final = layer_norm(own_rows + unit_share, normaliser_multipliers[1])
    own_emb = unit_vector(pool_images(image_final))
    picture_code_direction = lax.all_gather(own_emb, "mp", axis=0, tiled=True)
    text_normed = layer_norm(
        caption_closing_activations.astype(jnp.float32), normaliser_multipliers[2]
    ).astype(jnp.bfloat16)
    text_vector = jnp.dot(text_normed, caption_mapping_matrix, preferred_element_type=jnp.float32)
    caption_code_direction = unit_vector(text_vector)
    offset = lax.axis_index("dp") * picture_code_direction.shape[0]
    matching_scores = (
        sharpness_factor[0]
        * jnp.einsum(
            "pe,qe->pq",
            picture_code_direction,
            lax.all_gather(caption_code_direction, "dp", axis=0, tiled=True),
            preferred_element_type=jnp.float32,
        )
        + score_offset_term[0]
    )
    row_index = offset + lax.broadcasted_iota(jnp.int32, matching_scores.shape, 0)
    col_index = lax.broadcasted_iota(jnp.int32, matching_scores.shape, 1)
    labels = jnp.where(row_index == col_index, 1.0, -1.0).astype(jnp.float32)
    loss_terms = jax.nn.softplus(-labels * matching_scores)
    row_loss = jnp.sum(loss_terms, axis=1)
    col_loss = lax.psum_scatter(jnp.sum(loss_terms, axis=0), "dp", scatter_dimension=0, tiled=True)
    return (row_loss, col_loss)


def solution(mesh):
    return jax.shard_map(
        on_device,
        mesh=mesh,
        in_specs=(P("dp", None), P("dp", None), P(), P("dp", "mp"), P("mp", "dp"), P(), P(), P()),
        out_specs=(P("dp"), P("dp")),
        check_vma=False,
    )
```

profile of v0, /device:TPU:0, one launch (start us, length us, event | category | flops | bytes accessed | tf_op | source)
XLA Modules:
  0.0 232.3 jit_solution(16782825262965968562)
XLA Ops:
  7.2 0.0 copy-start
  7.2 0.0 all-gather.4.cloned.1.call-start
  7.2 0.7 all-gather.4.cloned.1.call-update
  7.9 0.0 all-gather.6.cloned.1.call-start
  8.0 0.7 all-gather.6.cloned.1.call-update
  8.7 0.0 reduce-scatter.2.cloned.1.call-start
  8.7 0.0 copy-start.1
  8.7 0.9 slice_reduce_fusion
  9.7 3.2 %convert_reduce_fusion = f32[2048]{0:T(1024)S(1)} fusion(bf16[2048,1152]{1,0:T(8,128)(2,1)} %param.8), kind=kLoop, calls=%fused_computation.12 | loop fusion | flops 4716544 | bytes 4726784 | tf_op jit(solution)/shard_map/reduce_sum | solution.py:10
  12.9 1.4 multiply_reduce_fusion
  14.3 53.6 %all-gather.4.cloned.1.call-done = bf16[1152,1076]{1,0:T(8,128)(2,1)} async-done(((bf16[144,1076]{1,0:T(8,128)(2,1)}), bf16[1152,1076]{1,0:T(8,128)(2,1)}) %all-gather.4.cloned.1.call-update) | async-done | bytes 2479120 | tf_op jit(solution)/shard_map/all_gather | solution.py:37
  67.9 55.8 %all-gather.6.cloned.1.call-done = bf16[1076,1152]{0,1:T(8,128)(2,1)} async-done(((bf16[1076,144]{0,1:T(8,128)(2,1)}), bf16[1076,1152]{0,1:T(8,128)(2,1)}) %all-gather.6.cloned.1.call-update) | async-done | bytes 2479120 | tf_op jit(solution)/shard_map/all_gather | solution.py:43
  123.7 20.0 %convolution_convert_fusion = bf16[2048,1152]{1,0:T(8,128)(2,1)} fusion(bf16[1076,1152]{0,1:T(8,128)(2,1)} %all-gather.6.cloned.1.call-done, bf16[1152,1076]{1,0:T(8,128)(2,1)} %all-gather.4.cloned.1.call-done, bf16[2048,1152]{1,0:T(8,128)(2,1)} %param.8, f32[1152]{0:T(1024)S(1)} %get-tuple-element.3, f32[2048]{0:T(1024)S(1)} %add_rsqrt_fusion, ...), kind=kOutput, calls=%fused_computation.11 | convolution fusion | flops 10188398592 | bytes 14416384 | tf_op jit(solution)/shard_map/dot_general | solution.py:41
  143.7 0.0 reduce-scatter.2.cloned.1.call-update
  143.7 0.0 copy-start.4
  143.8 7.9 %convert_element_type.27 = f32[2048,1152]{1,0:T(8,128)} convert(bf16[2048,1152]{1,0:T(8,128)(2,1)} %param.8) | non-fusion elementwise | flops 2359296 | bytes 14155776 | tf_op jit(solution)/shard_map/convert_element_type | solution.py:35
  153.0 0.6 dynamic-slice
  154.3 0.1 convert_reduce_fusion.1
  154.4 0.2 fusion.17
  154.6 0.6 multiply_reduce_fusion.2
  155.2 0.1 divide_convert_fusion
  155.3 30.6 %all_gather.15 = bf16[64,1152]{1,0:T(8,128)(2,1)S(1)} all-gather(bf16[8,1152]{1,0:T(8,128)(2,1)S(1)} %divide_convert_fusion), channel_id=1, replica_groups=mesh['dp'=8,'mp'=4] {'dp'}, dimensions={0}, use_global_device_ids=true | all-gather | bytes 165888 | tf_op jit(solution)/shard_map/all_gather | solution.py:66
  185.9 4.5 %reduce-scatter.2.cloned.1.call-done = bf16[512,1152]{1,0:T(8,128)(2,1)} async-done(((bf16[2048,1152]{1,0:T(8,128)(2,1)}), bf16[512,1152]{1,0:T(8,128)(2,1)}) %reduce-scatter.2.cloned.1.call-update) | async-done | bytes 1179664 | tf_op jit(solution)/shard_map/reduce_scatter | solution.py:46
  190.4 2.4 %fusion.14 = f32[512]{0:T(512)S(1)} fusion(bf16[512,1152]{1,0:T(8,128)(2,1)} %reduce-scatter.2.cloned.1.call-done, f32[2048,1152]{1,0:T(8,128)} %convert_element_type.27, s32[]{:T(128)S(6)} %select_n.12), kind=kLoop, calls=%fused_computation.24 | loop fusion | flops 1768960 | bytes 3540996 | tf_op jit(solution)/shard_map/reduce_sum | solution.py:10
  192.9 2.5 %multiply_reduce_fusion.1 = f32[512]{0:T(512)S(1)} fusion(f32[512]{0:T(512)S(1)} %broadcast_multiply_fusion.1, bf16[512,1152]{1,0:T(8,128)(2,1)} %reduce-scatter.2.cloned.1.call-done, f32[2048,1152]{1,0:T(8,128)} %convert_element_type.27, s32[]{:T(128)S(6)} %select_n.12), kind=kLoop, calls=%fused_computation.19 | loop fusion | flops 2948608 | bytes 3543044 | tf_op jit(solution)/shard_map/reduce_sum | solution.py:12
  195.4 2.2 bitcast_reduce_fusion
  197.6 0.1 multiply_reduce_fusion.3
  197.7 0.1 fusion.25
  197.8 5.2 %all-gather = bf16[4,2,1152]{2,1,0:T(2,128)(2,1)S(1)} all-gather(bf16[1,2,1152]{2,1,0:T(2,128)(2,1)S(1)} %fusion.25), channel_id=1, replica_groups=mesh['dp'=8,'mp'=4] {'mp'}, dimensions={0}, use_global_device_ids=true | all-gather | bytes 23040 | tf_op jit(solution)/shard_map/all_gather | solution.py:54
  203.0 0.8 fusion.30
  203.8 21.3 %all-reduce = f32[64]{0:T(128)S(1)} all-reduce(f32[64]{0:T(128)S(1)} %get-tuple-element.5), channel_id=3, replica_groups=mesh['dp'=8,'mp'=4] {'dp'}, use_global_device_ids=true, to_apply=%region_12.13.clone | all-reduce | flops 64 | bytes 512
  225.2 0.6 dynamic-slice.1
  (17 shorter events, 0.1 us)
Async XLA Ops:
  7.2 147.4 %copy-start = (bf16[1152,1152]{1,0:T(8,128)(2,1)S(1)}, bf16[1152,1152]{1,0:T(8,128)(2,1)}, u32[]{:S(2)}) copy-start(bf16[1152,1152]{1,0:T(8,128)(2,1)} %param.13) | copy-start | bytes 7962628
  7.2 60.7 %all-gather.4.cloned.1.call-start = ((), (), s32[]{:S(2)}) async-start(), calls=%async_computation.1 | async-start | bytes 2985984 | tf_op jit(solution)/shard_map/all_gather | solution.py:37
  7.9 115.7 %all-gather.6.cloned.1.call-start = ((), (), s32[]{:S(2)}) async-start(), calls=%async_computation.2 | async-start | bytes 2985984 | tf_op jit(solution)/shard_map/all_gather | solution.py:43
  8.7 181.8 %reduce-scatter.2.cloned.1.call-start = ((), (), s32[]{:S(2)}) async-start(), calls=%async_computation.3 | async-start | bytes 5898240 | tf_op jit(solution)/shard_map/reduce_scatter | solution.py:46
  8.7 4.2 %copy-start.1 = (bf16[2048,1152]{1,0:T(8,128)(2,1)S(1)}, bf16[2048,1152]{1,0:T(8,128)(2,1)}, u32[]{:S(2)}) copy-start(bf16[2048,1152]{1,0:T(8,128)(2,1)} %param.8) | copy-start | bytes 14155780
  143.7 9.3 %copy-start.4 = (u32[32]{0:T(128)S(1)}, u32[32]{0:T(128)}, u32[]{:S(2)}) copy-start(u32[32]{0:T(128)} %constant.53) | copy-start | bytes 388
  143.7 10.5 %copy-start.3 = (bf16[8,1152]{1,0:T(8,128)(2,1)S(1)}, bf16[8,1152]{1,0:T(8,128)(2,1)}, u32[]{:S(2)}) copy-start(bf16[8,1152]{1,0:T(8,128)(2,1)} %param.9) | copy-start | bytes 55300
  190.4 5.0 %copy-start.2 = (bf16[512,1152]{1,0:T(8,128)(2,1)S(1)}, bf16[512,1152]{1,0:T(8,128)(2,1)}, u32[]{:S(2)}) copy-start(bf16[512,1152]{1,0:T(8,128)(2,1)} %reduce-scatter.2.cloned.1.call-done) | copy-start | bytes 3538948
Sparse Core Ops, SparseCore 0:
  10.2 57.6 all-gather.3
  70.1 53.5 all-gather.5
  143.8 46.5 reduce-scatter.1
where the time goes:
time: 233 us; the launch traced here: 232 us
  waiting for transfers between devices  115 us (49%)
  blocking collectives  57.1 us (25%)
  matrix products  21.5 us (9%)
  other arithmetic  20.3 us (9%)
  between operations  15.8 us (7%)
    all_gather x1, waiting for transfers between devices, on_device(): lax.all_gather(contracting_matrix, 'dp', axis=1, tiled=True)  55.8 us
    all_gather x1, waiting for transfers between devices, on_device(): inner_weight = lax.all_gather(widening_matrix, 'dp', axis=0, tiled=True)  53.6 us
    all_gather x1, blocking collectives, on_device(): lax.all_gather(caption_code_direction, 'dp', axis=0, tiled=True)  30.6 us
    unnamed x1, blocking collectives  21.3 us
    dot_general x1, matrix products, on_device(): jnp.dot(image_units, lax.all_gather(contracting_matrix, 'dp', axis=1, til...  20 us
    convert_element_type x1, other arithmetic, on_device(): image_rows = picture_skip_activations.astype(jnp.float32)  7.92 us
    reduce_sum x3, other arithmetic, layer_norm(): average = jnp.mean(values, axis=-1, keepdims=True)  5.79 us
    all_gather x1, blocking collectives, on_device(): picture_code_direction = lax.all_gather(own_emb, 'mp', axis=0, tiled=True)  5.21 us
  transfers between devices with their start and end apart: 3, of which 3 were waited for; matrix products, arithmetic and copies ran while one was open for 7% of the time, Pallas kernels for 0%

commit v1 on v0

--- a/solution.py
+++ b/solution.py
@@ -4,6 +4,23 @@
 from jax.sharding import PartitionSpec as P
 
 PATCHES = 256
+
+
+def _time_loops(tile_in):
+    carry = jax.lax.axis_size("dp")
+    high, w2, block_out = (carry, jax.lax.axis_index("dp"), tile_in.shape[1])
+    mid_arr = jnp.zeros(
+        tuple((ix * high if u == 1 else ix for u, ix in enumerate(tile_in.shape))), tile_in.dtype
+    )
+    wide_out = lax.dynamic_update_slice_in_dim(mid_arr, tile_in, w2 * block_out, axis=1)
+    hop_no = 1
+    while hop_no < high:
+        tile_in = jax.lax.ppermute(tile_in, "dp", tuple(((u, (u + 1) % high) for u in range(high))))
+        wide_out = lax.dynamic_update_slice_in_dim(
+            wide_out, tile_in, (w2 - hop_no) % high * block_out, axis=1
+        )
+        hop_no += 1
+    return wide_out
 
 
 def layer_norm(values, norm_gain):
@@ -39,9 +56,7 @@
         jnp.dot(image_normed, inner_weight, preferred_element_type=jnp.float32), approximate=True
     ).astype(jnp.bfloat16)
     partial_out = jnp.dot(
-        image_units,
-        lax.all_gather(contracting_matrix, "dp", axis=1, tiled=True),
-        preferred_element_type=jnp.float32,
+        image_units, _time_loops(contracting_matrix), preferred_element_type=jnp.float32
     )
     unit_share = lax.psum_scatter(
         partial_out.astype(jnp.bfloat16), "mp", scatter_dimension=0, tiled=True

time: 233 us -> 217 us (0.931)
  waiting for transfers between devices: 115 us -> 87.8 us
  local copies, waits for them, and re-layouts: 2.17 us -> 11 us
  starting transfers between devices: 0.11 us -> 3.14 us
    ppermute x0 -> x7, waiting for transfers between devices: none -> 83.6 us  [_time_loops(): jax.lax.ppermute(tile_in, 'dp', tuple(((u, (u + 1) % high) for u in range...]
    all_gather x1 -> x0, waiting for transfers between devices: 55.8 us -> none  [on_device(): lax.all_gather(contracting_matrix, 'dp', axis=1, tiled=True)]
    all_gather x1, waiting for transfers between devices: 53.6 us -> 0.01 us  [on_device(): inner_weight = lax.all_gather(widening_matrix, 'dp', axis=0, tiled=True)]
    dynamic_update_slice x0 -> x8, local copies, waits for them, and re-layouts: none -> 7.98 us  [the longest x7 7.22 us: _time_loops(): lax.dynamic_update_slice_in_dim(wide_out, tile_in, (w2 - hop_no) % high *...]
    ppermute x0 -> x7, starting transfers between devices: none -> 3.06 us  [_time_loops(): jax.lax.ppermute(tile_in, 'dp', tuple(((u, (u + 1) % high) for u in range...]
  transfers between devices with their start and end apart: 3 -> 9, of which waited for: 3 -> 8; matrix products, arithmetic and copies ran while one was open for 7% -> 11% of each run, Pallas kernels for 0% -> 0%
where the time goes in v1:
time: 217 us; the launch traced here: 216 us
  waiting for transfers between devices  87.8 us (40%)
  blocking collectives  57.1 us (26%)
  matrix products  21.5 us (10%)
  other arithmetic  19.4 us (9%)
  between operations  16.3 us (8%)
  local copies, waits for them, and re-layouts  11 us (5%)
  starting transfers between devices  3.14 us (1%)
    ppermute x7, waiting for transfers between devices, _time_loops(): jax.lax.ppermute(tile_in, 'dp', tuple(((u, (u + 1) % high) for u in range...  83.6 us
    all_gather x1, blocking collectives, on_device(): lax.all_gather(caption_code_direction, 'dp', axis=0, tiled=True)  30.6 us
    unnamed x1, blocking collectives  21.3 us
    dot_general x1, matrix products, on_device(): jnp.dot(image_units, _time_loops(contracting_matrix), preferred_element_t...  20.1 us
    convert_element_type x1, other arithmetic, on_device(): image_rows = picture_skip_activations.astype(jnp.float32)  7.47 us
    dynamic_update_slice x7, local copies, waits for them, and re-layouts, _time_loops(): lax.dynamic_update_slice_in_dim(wide_out, tile_in, (w2 - hop_no) % high *...  7.22 us
    reduce_sum x3, other arithmetic, layer_norm(): average = jnp.mean(values, axis=-1, keepdims=True)  5.56 us
    all_gather x1, blocking collectives, on_device(): picture_code_direction = lax.all_gather(own_emb, 'mp', axis=0, tiled=True)  5.21 us
  transfers between devices with their start and end apart: 9, of which 8 were waited for; matrix products, arithmetic and copies ran while one was open for 11% of the time, Pallas kernels for 0%

profile of v1, /device:TPU:0, one launch (start us, length us, event | category | flops | bytes accessed | tf_op | source)
XLA Modules:
  0.0 216.1 jit_solution(6189891619524015564)
XLA Ops:
  7.2 0.7 all-gather.3.cloned.1.call-update
  8.0 3.0 %collective-permute-start = (bf16[1076,144]{0,1:T(8,128)(2,1)}, bf16[1076,144]{0,1:T(8,128)(2,1)S(1)}, u32[]{:S(2)}, u32[]{:S(2)}) collective-permute-start(bf16[1076,144]{0,1:T(8,128)(2,1)} %param.12), channel_id=1, source_target_pairs={{0,4},{4,8},{8,12},{12,16},{16,20},{20,24},{24,28},{28,0},{1,5},{5... | collective-permute-start | bytes 929672 | tf_op jit(solution)/shard_map/ppermute | solution.py:18
  11.0 11.0 %collective-permute-done = bf16[1076,144]{0,1:T(8,128)(2,1)S(1)} collective-permute-done((bf16[1076,144]{0,1:T(8,128)(2,1)}, bf16[1076,144]{0,1:T(8,128)(2,1)S(1)}, u32[]{:S(2)}, u32[]{:S(2)}) %collective-permute-start) | collective-permute-done | bytes 309920 | tf_op jit(solution)/shard_map/ppermute | solution.py:18
  22.1 3.0 %convert_reduce_fusion = f32[2048]{0:T(1024)S(1)} fusion(bf16[2048,1152]{1,0:T(8,128)(2,1)} %param.8), kind=kLoop, calls=%fused_computation.12 | loop fusion | flops 4716544 | bytes 4726784 | tf_op jit(solution)/shard_map/reduce_sum | solution.py:27
  25.1 16.9 %collective-permute-done.1 = bf16[1076,144]{0,1:T(8,128)(2,1)} collective-permute-done((bf16[1076,144]{0,1:T(8,128)(2,1)S(1)}, bf16[1076,144]{0,1:T(8,128)(2,1)}, u32[]{:S(2)}, u32[]{:S(2)}) %collective-permute-start.1) | collective-permute-done | bytes 309920 | tf_op jit(solution)/shard_map/ppermute | solution.py:18
  42.0 1.4 multiply_reduce_fusion
  43.6 10.6 %collective-permute-done.2 = bf16[1076,144]{0,1:T(8,128)(2,1)} collective-permute-done((bf16[1076,144]{0,1:T(8,128)(2,1)}, bf16[1076,144]{0,1:T(8,128)(2,1)}, u32[]{:S(2)}, u32[]{:S(2)}) %collective-permute-start.2) | collective-permute-done | bytes 309920 | tf_op jit(solution)/shard_map/ppermute | solution.py:18
  54.2 1.7 broadcast_in_dim.10
  56.0 0.8 constant_dynamic-update-slice_fusion.7
  56.7 16.5 %collective-permute-done.3 = bf16[1076,144]{0,1:T(8,128)(2,1)S(1)} collective-permute-done((bf16[1076,144]{0,1:T(8,128)(2,1)}, bf16[1076,144]{0,1:T(8,128)(2,1)S(1)}, u32[]{:S(2)}, u32[]{:S(2)}) %collective-permute-start.3) | collective-permute-done | bytes 309920 | tf_op jit(solution)/shard_map/ppermute | solution.py:18
  73.2 0.8 constant_dynamic-update-slice_fusion.6
  74.0 1.7 constant_dynamic-update-slice_fusion.5
  75.7 12.8 %collective-permute-done.4 = bf16[1076,144]{0,1:T(8,128)(2,1)S(1)} collective-permute-done((bf16[1076,144]{0,1:T(8,128)(2,1)S(1)}, bf16[1076,144]{0,1:T(8,128)(2,1)S(1)}, u32[]{:S(2)}, u32[]{:S(2)}) %collective-permute-start.4) | collective-permute-done | bytes 309920 | tf_op jit(solution)/shard_map/ppermute | solution.py:18
  88.5 1.7 constant_dynamic-update-slice_fusion.4
  90.2 0.7 constant_dynamic-update-slice_fusion.3
  91.0 7.5 %collective-permute-done.5 = bf16[1076,144]{0,1:T(8,128)(2,1)S(1)} collective-permute-done((bf16[1076,144]{0,1:T(8,128)(2,1)S(1)}, bf16[1076,144]{0,1:T(8,128)(2,1)S(1)}, u32[]{:S(2)}, u32[]{:S(2)}) %collective-permute-start.5) | collective-permute-done | bytes 309920 | tf_op jit(solution)/shard_map/ppermute | solution.py:18
  98.4 0.8 constant_dynamic-update-slice_fusion.2
  99.2 0.7 constant_dynamic-update-slice_fusion.1
  99.9 8.3 %collective-permute-done.6 = bf16[1076,144]{0,1:T(8,128)(2,1)S(1)} collective-permute-done((bf16[1076,144]{0,1:T(8,128)(2,1)S(1)}, bf16[1076,144]{0,1:T(8,128)(2,1)S(1)}, u32[]{:S(2)}, u32[]{:S(2)}) %collective-permute-start.6) | collective-permute-done | bytes 309920 | tf_op jit(solution)/shard_map/ppermute | solution.py:18
  108.2 0.8 constant_dynamic-update-slice_fusion
  109.0 20.1 %convolution_convert_fusion = bf16[2048,1152]{1,0:T(8,128)(2,1)} fusion(bf16[1076,1152]{0,1:T(8,128)(2,1)} %constant_dynamic-update-slice_fusion, bf16[1152,1076]{1,0:T(8,128)(2,1)} %all-gather.3.cloned.1.call-done, bf16[2048,1152]{1,0:T(8,128)(2,1)} %param.8, f32[1152]{0:T(1024)S(1)} %get-tuple-element.3, f32[2048]{0:T(1024)S(1)} %add_rsqrt_fusion, ...), kind=kOutput, calls=%fused_computation.11 | convolution fusion | flops 10188398592 | bytes 14416384 | tf_op jit(solution)/shard_map/dot_general | solution.py:58
  129.1 7.5 %convert_element_type.27 = f32[2048,1152]{1,0:T(8,128)} convert(bf16[2048,1152]{1,0:T(8,128)(2,1)} %param.8) | non-fusion elementwise | flops 2359296 | bytes 14155776 | tf_op jit(solution)/shard_map/convert_element_type | solution.py:52
  139.5 0.6 multiply_reduce_fusion.2
  140.2 30.6 %all_gather.11 = bf16[64,1152]{1,0:T(8,128)(2,1)S(1)} all-gather(bf16[8,1152]{1,0:T(8,128)(2,1)S(1)} %divide_convert_fusion), channel_id=1, replica_groups=mesh['dp'=8,'mp'=4] {'dp'}, dimensions={0}, use_global_device_ids=true | all-gather | bytes 165888 | tf_op jit(solution)/shard_map/all_gather | solution.py:81
  170.8 3.5 %reduce-scatter.2.cloned.1.call-done = bf16[512,1152]{1,0:T(8,128)(2,1)} async-done(((bf16[2048,1152]{1,0:T(8,128)(2,1)}), bf16[512,1152]{1,0:T(8,128)(2,1)}) %reduce-scatter.2.cloned.1.call-update) | async-done | bytes 1179664 | tf_op jit(solution)/shard_map/reduce_scatter | solution.py:61
  174.2 2.4 %fusion.14 = f32[512]{0:T(512)S(1)} fusion(bf16[512,1152]{1,0:T(8,128)(2,1)} %reduce-scatter.2.cloned.1.call-done, f32[2048,1152]{1,0:T(8,128)} %convert_element_type.27, s32[]{:T(128)S(6)} %select_n.67), kind=kLoop, calls=%fused_computation.24 | loop fusion | flops 1768960 | bytes 3540996 | tf_op jit(solution)/shard_map/reduce_sum | solution.py:27
  176.7 2.2 %multiply_reduce_fusion.1 = f32[512]{0:T(512)S(1)} fusion(f32[512]{0:T(512)S(1)} %broadcast_multiply_fusion.1, bf16[512,1152]{1,0:T(8,128)(2,1)S(1)} %copy-done.2, f32[2048,1152]{1,0:T(8,128)} %convert_element_type.27, s32[]{:T(128)S(6)} %select_n.67), kind=kLoop, calls=%fused_computation.19 | loop fusion | flops 2948608 | bytes 3543044 | tf_op jit(solution)/shard_map/reduce_sum | solution.py:29
  178.9 2.2 %bitcast_reduce_fusion = f32[2,1152]{1,0:T(2,128)S(1)} fusion(f32[1152]{0:T(1024)S(1)} %get-tuple-element.4, f32[512]{0:T(512)S(1)} %add_rsqrt_fusion.1, f32[512]{0:T(512)S(1)} %broadcast_multiply_fusion.1, bf16[512,1152]{1,0:T(8,128)(2,1)S(1)} %copy-done.2, f32[2048,1152]{1,0:T(8,128)} %convert_element_type.27, s32[]{:T(128)S(6)} %select_n.67), kind=kLoop, calls=%fused_computation.17 | loop fusion | flops 3536640 | bytes 3556868 | tf_op jit(solution)/shard_map/reduce_sum | solution.py:39
  181.3 5.2 %all-gather = bf16[4,2,1152]{2,1,0:T(2,128)(2,1)S(1)} all-gather(bf16[1,2,1152]{2,1,0:T(2,128)(2,1)S(1)} %fusion.25), channel_id=1, replica_groups=mesh['dp'=8,'mp'=4] {'mp'}, dimensions={0}, use_global_device_ids=true | all-gather | bytes 23040 | tf_op jit(solution)/shard_map/all_gather | solution.py:69
  186.6 0.8 fusion.30
  187.4 21.3 %all-reduce = f32[64]{0:T(128)S(1)} all-reduce(f32[64]{0:T(128)S(1)} %get-tuple-element.5), channel_id=3, replica_groups=mesh['dp'=8,'mp'=4] {'dp'}, use_global_device_ids=true, to_apply=%region_12.13.clone | all-reduce | flops 64 | bytes 512
  208.7 0.6 dynamic-slice.1
  (41 shorter events, 1.4 us)
Async XLA Ops:
  7.2 132.3 %copy-start = (bf16[1152,1152]{1,0:T(8,128)(2,1)S(1)}, bf16[1152,1152]{1,0:T(8,128)(2,1)}, u32[]{:S(2)}) copy-start(bf16[1152,1152]{1,0:T(8,128)(2,1)} %param.13) | copy-start | bytes 7962628
  7.2 101.8 %all-gather.3.cloned.1.call-start = ((), (), s32[]{:S(2)}) async-start(), calls=%async_computation.1 | async-start | bytes 2985984 | tf_op jit(solution)/shard_map/all_gather | solution.py:54
  7.9 166.3 %reduce-scatter.2.cloned.1.call-start = ((), (), s32[]{:S(2)}) async-start(), calls=%async_computation.2 | async-start | bytes 5898240 | tf_op jit(solution)/shard_map/reduce_scatter | solution.py:61
  8.0 34.1 %copy-start.1 = (bf16[2048,1152]{1,0:T(8,128)(2,1)S(1)}, bf16[2048,1152]{1,0:T(8,128)(2,1)}, u32[]{:S(2)}) copy-start(bf16[2048,1152]{1,0:T(8,128)(2,1)} %param.8) | copy-start | bytes 14155780
  8.0 14.1 %collective-permute-start = (bf16[1076,144]{0,1:T(8,128)(2,1)}, bf16[1076,144]{0,1:T(8,128)(2,1)S(1)}, u32[]{:S(2)}, u32[]{:S(2)}) collective-permute-start(bf16[1076,144]{0,1:T(8,128)(2,1)} %param.12), channel_id=1, source_target_pairs={{0,4},{4,8},{8,12},{12,16},{16,20},{20,24},{24,28},{28,0},{1,5},{5... | collective-permute-start | bytes 929672 | tf_op jit(solution)/shard_map/ppermute | solution.py:18
  22.1 19.9 %collective-permute-start.1 = (bf16[1076,144]{0,1:T(8,128)(2,1)S(1)}, bf16[1076,144]{0,1:T(8,128)(2,1)}, u32[]{:S(2)}, u32[]{:S(2)}) collective-permute-start(bf16[1076,144]{0,1:T(8,128)(2,1)S(1)} %collective-permute-done), channel_id=1, source_target_pairs={{0,4},{4,8},{8,12},{12,16},{16,20},{20,24},{24,28},{28,0},{1,5},{5... | collective-permute-start | bytes 929672 | tf_op jit(solution)/shard_map/ppermute | solution.py:18
  25.1 29.1 %copy-start.5 = (f32[3,1152]{1,0:T(4,128)S(1)}, f32[3,1152]{1,0:T(4,128)}, u32[]{:S(2)}) copy-start(f32[3,1152]{1,0:T(4,128)} %param.10) | copy-start | bytes 41476
  42.0 12.2 %collective-permute-start.2 = (bf16[1076,144]{0,1:T(8,128)(2,1)}, bf16[1076,144]{0,1:T(8,128)(2,1)}, u32[]{:S(2)}, u32[]{:S(2)}) collective-permute-start(bf16[1076,144]{0,1:T(8,128)(2,1)} %collective-permute-done.1), channel_id=1, source_target_pairs={{0,4},{4,8},{8,12},{12,16},{16,20},{20,24},{24,28},{28,0},{1,5},{5... | collective-permute-start | bytes 929672 | tf_op jit(solution)/shard_map/ppermute | solution.py:18
  43.4 12.6 %copy-start.3 = (bf16[1076,144]{0,1:T(8,128)(2,1)S(1)}, bf16[1076,144]{0,1:T(8,128)(2,1)}, u32[]{:S(2)}) copy-start(bf16[1076,144]{0,1:T(8,128)(2,1)} %param.12) | copy-start | bytes 929668
  54.2 19.0 %collective-permute-start.3 = (bf16[1076,144]{0,1:T(8,128)(2,1)}, bf16[1076,144]{0,1:T(8,128)(2,1)S(1)}, u32[]{:S(2)}, u32[]{:S(2)}) collective-permute-start(bf16[1076,144]{0,1:T(8,128)(2,1)} %collective-permute-done.2), channel_id=1, source_target_pairs={{0,4},{4,8},{8,12},{12,16},{16,20},{20,24},{24,28},{28,0},{1,5},{5... | collective-permute-start | bytes 929672 | tf_op jit(solution)/shard_map/ppermute | solution.py:18
  73.2 15.3 %collective-permute-start.4 = (bf16[1076,144]{0,1:T(8,128)(2,1)S(1)}, bf16[1076,144]{0,1:T(8,128)(2,1)S(1)}, u32[]{:S(2)}, u32[]{:S(2)}) collective-permute-start(bf16[1076,144]{0,1:T(8,128)(2,1)S(1)} %collective-permute-done.3), channel_id=1, source_target_pairs={{0,4},{4,8},{8,12},{12,16},{16,20},{20,24},{24,28},{28,0},{1,5},{5... | collective-permute-start | bytes 929672 | tf_op jit(solution)/shard_map/ppermute | solution.py:18
  88.5 9.9 %collective-permute-start.5 = (bf16[1076,144]{0,1:T(8,128)(2,1)S(1)}, bf16[1076,144]{0,1:T(8,128)(2,1)S(1)}, u32[]{:S(2)}, u32[]{:S(2)}) collective-permute-start(bf16[1076,144]{0,1:T(8,128)(2,1)S(1)} %collective-permute-done.4), channel_id=1, source_target_pairs={{0,4},{4,8},{8,12},{12,16},{16,20},{20,24},{24,28},{28,0},{1,5},{5... | collective-permute-start | bytes 929672 | tf_op jit(solution)/shard_map/ppermute | solution.py:18
  98.4 9.8 %collective-permute-start.6 = (bf16[1076,144]{0,1:T(8,128)(2,1)S(1)}, bf16[1076,144]{0,1:T(8,128)(2,1)S(1)}, u32[]{:S(2)}, u32[]{:S(2)}) collective-permute-start(bf16[1076,144]{0,1:T(8,128)(2,1)S(1)} %collective-permute-done.5), channel_id=1, source_target_pairs={{0,4},{4,8},{8,12},{12,16},{16,20},{20,24},{24,28},{28,0},{1,5},{5... | collective-permute-start | bytes 929672 | tf_op jit(solution)/shard_map/ppermute | solution.py:18
  129.1 8.8 %copy-start.6 = (u32[32]{0:T(128)S(1)}, u32[32]{0:T(128)}, u32[]{:S(2)}) copy-start(u32[32]{0:T(128)} %constant.114) | copy-start | bytes 388
  129.1 10.0 %copy-start.4 = (bf16[8,1152]{1,0:T(8,128)(2,1)S(1)}, bf16[8,1152]{1,0:T(8,128)(2,1)}, u32[]{:S(2)}) copy-start(bf16[8,1152]{1,0:T(8,128)(2,1)} %param.9) | copy-start | bytes 55300
  174.2 2.4 %copy-start.2 = (bf16[512,1152]{1,0:T(8,128)(2,1)S(1)}, bf16[512,1152]{1,0:T(8,128)(2,1)}, u32[]{:S(2)}) copy-start(bf16[512,1152]{1,0:T(8,128)(2,1)} %reduce-scatter.2.cloned.1.call-done) | copy-start | bytes 3538948
Sparse Core Ops, SparseCore 0:
  10.2 72.1 all-gather.2
  129.2 44.9 reduce-scatter.1
